TPU v7x, 32 devices: a whole 2x2x4 slice. The times are simulated.
32 devices in a mesh: seq: 16 (over z, y, x), bat: 2 (over core).
Axes of the slice: x: 2, y: 2, z: 4, core: 2. Of those that a mesh axis runs over, the one named last changes fastest.
Arguments:
- tokens: bfloat16 [2, 65536, 256], P('bat', 'seq'), may hold values from -6 to 6
- filter_spectrum: bfloat16 [2, 256, 256, 256], P(None, 'seq', None, 'bat'), may hold values from -6 to 6
- skip_gain: float32 [256], replicated, may hold values from 0.5 to 1.5
Outputs:
- mixed: bfloat16 [2, 65536, 256], P('bat', 'seq')
All inputs are finite; a program needn't handle non-finite values.
Results may differ from a plain program's by a relative error of at most 0.012.
Values may be sent and summed in bfloat16 or wider, within the bound.
A program may use at most 64 MiB of HBM per device.

v0:
```python
import math
import jax
import jax.numpy as jnp
from jax import lax
from jax.sharding import PartitionSpec as P

N1 = 256
N2 = 256


def cos_sin(points):
    steps_range = jnp.arange(points, dtype=jnp.int32)
    index_grid = steps_range[:, None] * steps_range[None, :] % points
    phase_angle = index_grid.astype(jnp.float32) * (2.0 * math.pi / points)
    return (jnp.cos(phase_angle), jnp.sin(phase_angle))


def real_table(points):
    cosine, sine_vals = cos_sin(points)
    return jnp.stack([cosine, -sine_vals], axis=1).astype(jnp.bfloat16)


def complex_table(points, signum, factor):
    cosine, sine_vals = cos_sin(points)
    top_rows = jnp.stack([cosine, signum * sine_vals], axis=1)
    low_rows = jnp.stack([-signum * sine_vals, cosine], axis=1)
    return (jnp.stack([top_rows, low_rows], axis=0) * factor).astype(jnp.bfloat16)


def final_table(points):
    cosine, sine_vals = cos_sin(points)
    return (jnp.stack([cosine, -sine_vals], axis=0) / points).astype(jnp.bfloat16)


def twiddle_phase(first_rows, second_rows, period):
    index_grid = first_rows[:, None] * second_rows[None, :] % period
    phase_angle = index_grid.astype(jnp.float32) * (2.0 * math.pi / period)
    return (jnp.cos(phase_angle)[..., None], jnp.sin(phase_angle)[..., None])


def multiply(values, filters):
    chosen = values.astype(jnp.float32)
    weights = lax.all_gather(filters, "bat", axis=3, tiled=True).astype(jnp.float32)[:, None]
    real_part = chosen[0] * weights[0] - chosen[1] * weights[1]
    imag_part = chosen[0] * weights[1] + chosen[1] * weights[0]
    return jnp.stack([real_part, imag_part]).astype(jnp.bfloat16)


def body(tokens, filter_spectrum, skip_gain):
    seq_count = lax.axis_size("seq")
    device_index = lax.axis_index("seq")
    batch_rows, local_length, channels = tokens.shape
    rows_local = N1 // seq_count
    cols_local = N2 // seq_count
    period = N1 * N2
    laid_out = tokens.reshape(batch_rows, rows_local, N2, channels)
    columns = lax.all_to_all(laid_out, "seq", split_axis=2, concat_axis=1, tiled=True)
    first_section = jnp.einsum(
        "bnmc,nsk->sbkmc", columns, real_table(N1), preferred_element_type=jnp.float32
    )
    own_cols = device_index * cols_local + jnp.arange(cols_local, dtype=jnp.int32)
    cos_tw, sin_tw = twiddle_phase(jnp.arange(N1, dtype=jnp.int32), own_cols, period)
    real_part = first_section[0] * cos_tw + first_section[1] * sin_tw
    imag_part = first_section[1] * cos_tw - first_section[0] * sin_tw
    turned = jnp.stack([real_part, imag_part]).astype(jnp.bfloat16)
    rows_block = lax.all_to_all(turned, "seq", split_axis=2, concat_axis=3, tiled=True)
    spectrum = jnp.einsum(
        "rbknc,rnsj->sbkjc",
        rows_block,
        complex_table(N2, -1.0, 1.0),
        preferred_element_type=jnp.float32,
    ).astype(jnp.bfloat16)
    product = multiply(spectrum, filter_spectrum)
    back_section = jnp.einsum(
        "rbkjc,rjsn->sbknc",
        product,
        complex_table(N2, 1.0, 1.0 / N2),
        preferred_element_type=jnp.float32,
    )
    own_rows = device_index * rows_local + jnp.arange(rows_local, dtype=jnp.int32)
    cos_back, sin_back = twiddle_phase(own_rows, jnp.arange(N2, dtype=jnp.int32), period)
    real_back = back_section[0] * cos_back - back_section[1] * sin_back
    imag_back = back_section[0] * sin_back + back_section[1] * cos_back
    turned_back = jnp.stack([real_back, imag_back]).astype(jnp.bfloat16)
    mixed_cols = lax.all_to_all(turned_back, "seq", split_axis=3, concat_axis=2, tiled=True)
    filtered = jnp.einsum(
        "rbknc,rkm->bmnc", mixed_cols, final_table(N1), preferred_element_type=jnp.float32
    )
    result = (filtered + skip_gain * columns.astype(jnp.float32)).astype(jnp.bfloat16)
    restored = lax.all_to_all(result, "seq", split_axis=1, concat_axis=2, tiled=True)
    return restored.reshape(batch_rows, local_length, channels)


def solution(mesh):
    placed = (P("bat", "seq", None), P(None, "seq", None, "bat"), P())
    return jax.shard_map(
        body, mesh=mesh, in_specs=placed, out_specs=P("bat", "seq", None), check_vma=False
    )
```

profile of v0, /device:TPU:0, one launch (start us, length us, event | category | flops | bytes accessed | tf_op | source)
XLA Modules:
  0.0 355.4 jit_solution(5459308199365572002)
XLA Ops:
  6.5 4.1 %copy.31 = bf16[1,16,256,256]{3,1,0,2:T(8,128)(2,1)} copy(bf16[1,16,256,256]{3,2,1,0:T(8,128)(2,1)} %bitcast.109) | data formatting | bytes 4194304 | tf_op jit(solution)/shard_map/reshape | solution.py:56
  10.6 8.3 %all-to-all-start = ((bf16[1,16,256,256]{3,1,0,2:T(8,128)(2,1)}), bf16[1,16,256,256]{3,1,0,2:T(8,128)(2,1)S(1)}, u32[]{:S(2)}, u32[]{:S(2)}) async-start(bf16[1,16,256,256]{3,1,0,2:T(8,128)(2,1)} %copy.31), calls=%async_computation | async-start | bytes 4194304 | tf_op jit(solution)/shard_map/all_to_all | solution.py:57
  19.0 1.1 negate_convert_fusion
  20.1 0.2 fusion.57
  20.2 41.8 %all-to-all-done = bf16[1,16,256,256]{3,1,0,2:T(8,128)(2,1)S(1)} async-done(((bf16[1,16,256,256]{3,1,0,2:T(8,128)(2,1)}), bf16[1,16,256,256]{3,1,0,2:T(8,128)(2,1)S(1)}, u32[]{:S(2)}, u32[]{:S(2)}) %all-to-all-start) | async-done | bytes 2097184 | tf_op jit(solution)/shard_map/all_to_all | solution.py:57
  62.0 0.7 copy.32
  62.7 1.2 copy.33
  63.9 1.3 fusion.18
  65.2 1.5 fusion.8
  66.6 0.4 pad_maximum_fusion
  67.0 4.3 %copy.34 = bf16[2,1,256,16,256]{4,3,1,0,2:T(8,128)(2,1)} copy(bf16[2,1,256,16,256]{4,2,3,1,0:T(8,128)(2,1)S(1)} %pad_maximum_fusion) | data formatting | bytes 8388608 | tf_op jit(solution)/shard_map/stack | solution.py:65
  71.3 10.1 %all-to-all-start.1 = ((bf16[2,1,256,16,256]{4,3,1,0,2:T(8,128)(2,1)}), bf16[2,1,256,16,256]{4,3,1,0,2:T(8,128)(2,1)}, u32[]{:S(2)}, u32[]{:S(2)}) async-start(bf16[2,1,256,16,256]{4,3,1,0,2:T(8,128)(2,1)} %copy.34), calls=%async_computation.1 | async-start | bytes 8388608 | tf_op jit(solution)/shard_map/all_to_all | solution.py:66
  81.4 0.2 all-gather.2.cloned.1.call-start
  81.6 0.5 all-gather.2.cloned.1.call-update
  82.1 1.0 fusion.38
  83.1 1.0 fusion.37
  84.1 1.0 broadcast_multiply_fusion
  85.1 0.1 fusion.16
  85.1 0.9 maximum_bitcast_fusion
  86.0 0.2 fusion.55
  86.2 11.6 %all-gather.2.cloned.1.call-done = bf16[2,16,256,256]{3,2,1,0:T(8,128)(2,1)} async-done(((bf16[2,16,256,128]{3,2,1,0:T(8,128)(2,1)}), bf16[2,16,256,256]{3,2,1,0:T(8,128)(2,1)}) %all-gather.2.cloned.1.call-update) | async-done | bytes 4194320 | tf_op jit(solution)/shard_map/all_gather | solution.py:43
  97.8 6.5 %convert_element_type.144 = f32[2,16,256,256]{3,2,1,0:T(8,128)} convert(bf16[2,16,256,256]{3,2,1,0:T(8,128)(2,1)} %all-gather.2.cloned.1.call-done) | non-fusion elementwise | flops 2097152 | bytes 12582912 | tf_op jit(solution)/shard_map/convert_element_type | solution.py:43
  104.3 55.5 %all-to-all-done.1 = bf16[2,1,256,16,256]{4,3,1,0,2:T(8,128)(2,1)} async-done(((bf16[2,1,256,16,256]{4,3,1,0,2:T(8,128)(2,1)}), bf16[2,1,256,16,256]{4,3,1,0,2:T(8,128)(2,1)}, u32[]{:S(2)}, u32[]{:S(2)}) %all-to-all-start.1) | async-done | bytes 4194336 | tf_op jit(solution)/shard_map/all_to_all | solution.py:66
  159.8 2.7 copy.35
  162.5 0.0 slice-start
  162.5 0.0 slice-start.1
  162.5 2.4 convert_bitcast_fusion.1
  164.9 0.0 slice-done
  164.9 1.1 slice-done.1
  166.0 0.0 copy-start
  166.0 1.8 subtract_convert_fusion.1
  167.8 0.0 copy-done
  167.8 2.4 fusion.5
  170.2 1.5 subtract_convert_fusion
  171.6 0.4 pad_maximum_fusion.2
  172.0 4.4 %copy.40 = bf16[2,1,16,256,256]{4,2,0,1,3:T(8,128)(2,1)} copy(bf16[2,1,16,256,256]{4,3,2,0,1:T(8,128)(2,1)S(1)} %pad_maximum_fusion.2) | data formatting | bytes 8388608 | tf_op jit(solution)/shard_map/stack | solution.py:84
  176.4 19.4 %all-to-all-start.2 = ((bf16[2,1,16,256,256]{4,2,0,1,3:T(8,128)(2,1)}), bf16[2,1,16,256,256]{4,2,0,1,3:T(8,128)(2,1)}, u32[]{:S(2)}, u32[]{:S(2)}) async-start(bf16[2,1,16,256,256]{4,2,0,1,3:T(8,128)(2,1)} %copy.40), calls=%async_computation.2 | async-start | bytes 8388608 | tf_op jit(solution)/shard_map/all_to_all | solution.py:85
  195.8 1.0 sine_negate_fusion
  196.9 77.4 %all-to-all-done.2 = bf16[2,1,16,256,256]{4,2,0,1,3:T(8,128)(2,1)} async-done(((bf16[2,1,16,256,256]{4,2,0,1,3:T(8,128)(2,1)}), bf16[2,1,16,256,256]{4,2,0,1,3:T(8,128)(2,1)}, u32[]{:S(2)}, u32[]{:S(2)}) %all-to-all-start.2) | async-done | bytes 4194336 | tf_op jit(solution)/shard_map/all_to_all | solution.py:85
  274.3 0.0 copy-start.1
  274.3 2.7 copy.41
  277.0 0.0 copy-done.1
  277.0 1.3 fusion.10
  278.4 1.2 copy.42
  279.6 67.4 %all_to_all.60 = bf16[1,256,16,256]{3,2,0,1:T(8,128)(2,1)S(1)} all-to-all(bf16[1,256,16,256]{3,2,0,1:T(8,128)(2,1)S(1)} %copy.42), channel_id=1, replica_groups=mesh['seq'=16,'bat'=2] {'seq'}, dimensions={1} | all-to-all | bytes 4194304 | tf_op jit(solution)/shard_map/all_to_all | solution.py:90
  347.0 1.5 copy.43
  (2 shorter events, 0.0 us)
Async XLA Ops:
  10.6 51.4 %all-to-all-start = ((bf16[1,16,256,256]{3,1,0,2:T(8,128)(2,1)}), bf16[1,16,256,256]{3,1,0,2:T(8,128)(2,1)S(1)}, u32[]{:S(2)}, u32[]{:S(2)}) async-start(bf16[1,16,256,256]{3,1,0,2:T(8,128)(2,1)} %copy.31), calls=%async_computation | async-start | bytes 4194304 | tf_op jit(solution)/shard_map/all_to_all | solution.py:57
  71.3 88.5 %all-to-all-start.1 = ((bf16[2,1,256,16,256]{4,3,1,0,2:T(8,128)(2,1)}), bf16[2,1,256,16,256]{4,3,1,0,2:T(8,128)(2,1)}, u32[]{:S(2)}, u32[]{:S(2)}) async-start(bf16[2,1,256,16,256]{4,3,1,0,2:T(8,128)(2,1)} %copy.34), calls=%async_computation.1 | async-start | bytes 8388608 | tf_op jit(solution)/shard_map/all_to_all | solution.py:66
  81.4 16.4 %all-gather.2.cloned.1.call-start = ((), (), s32[]{:S(2)}) async-start(), calls=%async_computation.4 | async-start | bytes 6291456 | tf_op jit(solution)/shard_map/all_gather | solution.py:43
  162.5 2.4 slice-start
  162.5 3.5 slice-start.1
  166.0 1.8 copy-start
  176.4 97.9 %all-to-all-start.2 = ((bf16[2,1,16,256,256]{4,2,0,1,3:T(8,128)(2,1)}), bf16[2,1,16,256,256]{4,2,0,1,3:T(8,128)(2,1)}, u32[]{:S(2)}, u32[]{:S(2)}) async-start(bf16[2,1,16,256,256]{4,2,0,1,3:T(8,128)(2,1)} %copy.40), calls=%async_computation.2 | async-start | bytes 8388608 | tf_op jit(solution)/shard_map/all_to_all | solution.py:85
  274.3 2.8 copy-start.1
Sparse Core Ops, SparseCore 0:
  83.7 13.9 all-gather.1
where the time goes:
time: 356 us; the launch traced here: 355 us
  waiting for transfers between devices  187 us (53%)
  blocking collectives  67.4 us (19%)
  starting transfers between devices  38 us (11%)
  local copies, waits for them, and re-layouts  24 us (7%)
  other arithmetic  18.3 us (5%)
  between operations  13.6 us (4%)
  matrix products  7.29 us (2%)
    all_to_all x1, waiting for transfers between devices, body(): lax.all_to_all(turned_back, 'seq', split_axis=3, concat_axis=2, tiled=True)  77.4 us
    all_to_all x1, blocking collectives, body(): lax.all_to_all(result, 'seq', split_axis=1, concat_axis=2, tiled=True)  67.4 us
    all_to_all x1, waiting for transfers between devices, body(): lax.all_to_all(turned, 'seq', split_axis=2, concat_axis=3, tiled=True)  55.5 us
    all_to_all x1, waiting for transfers between devices, body(): lax.all_to_all(laid_out, 'seq', split_axis=2, concat_axis=1, tiled=True)  41.8 us
    all_to_all x1, starting transfers between devices, body(): lax.all_to_all(turned_back, 'seq', split_axis=3, concat_axis=2, tiled=True)  19.4 us
    all_gather x1, waiting for transfers between devices, multiply(): lax.all_gather(filters, 'bat', axis=3, tiled=True).astype(jnp.float32)  11.6 us
    all_to_all x1, starting transfers between devices, body(): lax.all_to_all(turned, 'seq', split_axis=2, concat_axis=3, tiled=True)  10.1 us
    all_to_all x1, starting transfers between devices, body(): lax.all_to_all(laid_out, 'seq', split_axis=2, concat_axis=1, tiled=True)  8.34 us
  transfers between devices with their start and end apart: 4, of which 4 were waited for; matrix products, arithmetic and copies ran while one was open for 4% of the time, Pallas kernels for 0%

commit v1 on v0

--- a/solution.py
+++ b/solution.py
@@ -63,7 +63,10 @@
     real_part = first_section[0] * cos_tw + first_section[1] * sin_tw
     imag_part = first_section[1] * cos_tw - first_section[0] * sin_tw
     turned = jnp.stack([real_part, imag_part]).astype(jnp.bfloat16)
-    rows_block = lax.all_to_all(turned, "seq", split_axis=2, concat_axis=3, tiled=True)
+    rows_block = jnp.concatenate(
+        lax.all_to_all(jnp.stack(jnp.split(turned, lax.axis_size("seq"), axis=2)), "seq", 0, 0),
+        axis=3,
+    )
     spectrum = jnp.einsum(
         "rbknc,rnsj->sbkjc",
         rows_block,

time: 356 us -> 370 us (1.039)
  local copies, waits for them, and re-layouts: 24 us -> 32.3 us
  matrix products: 7.29 us -> 11.4 us
    unnamed x8 -> x21, local copies, waits for them, and re-layouts: 1.09 us -> 10.8 us
    reshape x0 -> x1, local copies, waits for them, and re-layouts: none -> 5.65 us  [body(): jnp.concatenate(lax.all_to_all(jnp.stack(jnp.split(turned, lax.axis_size(...]
    another operation x1 -> x0, local copies, waits for them, and re-layouts: 4.31 us -> none  [body(): turned = jnp.stack([real_part, imag_part]).astype(jnp.bfloat16)]
  transfers between devices with their start and end apart: 4 -> 4, of which waited for: 4 -> 4; matrix products, arithmetic and copies ran while one was open for 4% -> 3% of each run, Pallas kernels for 0% -> 0%
where the time goes in v1:
time: 370 us
  waiting for transfers between devices  187 us (51%)
  blocking collectives  67.5 us (18%)
  starting transfers between devices  38 us (10%)
  local copies, waits for them, and re-layouts  32.3 us (9%)
  other arithmetic  20.2 us (5%)
  between operations  13.6 us (4%)
  matrix products  11.4 us (3%)
    all_to_all x1, waiting for transfers between devices, body(): lax.all_to_all(turned_back, 'seq', split_axis=3, concat_axis=2, tiled=True)  77.4 us
    all_to_all x1, blocking collectives, body(): lax.all_to_all(result, 'seq', split_axis=1, concat_axis=2, tiled=True)  67.5 us
    all_to_all x1, waiting for transfers between devices, body(): lax.all_to_all(jnp.stack(jnp.split(turned, lax.axis_size('seq'), axis=2))...  55.5 us
    all_to_all x1, waiting for transfers between devices, body(): lax.all_to_all(laid_out, 'seq', split_axis=2, concat_axis=1, tiled=True)  41.8 us
    all_to_all x1, starting transfers between devices, body(): lax.all_to_all(turned_back, 'seq', split_axis=3, concat_axis=2, tiled=True)  19.4 us
    all_gather x1, waiting for transfers between devices, multiply(): lax.all_gather(filters, 'bat', axis=3, tiled=True).astype(jnp.float32)  11.6 us
    unnamed x21, local copies, waits for them, and re-layouts  10.8 us
    all_to_all x1, starting transfers between devices, body(): lax.all_to_all(jnp.stack(jnp.split(turned, lax.axis_size('seq'), axis=2))...  10.1 us
  transfers between devices with their start and end apart: 4, of which 4 were waited for; matrix products, arithmetic and copies ran while one was open for 3% of the time, Pallas kernels for 0%

profile of v1, /device:TPU:0, one launch (start us, length us, event | category | flops | bytes accessed | tf_op | source)
XLA Modules:
  0.0 369.7 jit_solution(15648905718847209327)
XLA Ops:
  6.5 4.1 %copy.76 = bf16[1,16,256,256]{3,1,0,2:T(8,128)(2,1)} copy(bf16[1,16,256,256]{3,2,1,0:T(8,128)(2,1)} %bitcast.189) | data formatting | bytes 4194304 | tf_op jit(solution)/shard_map/reshape | solution.py:56
  10.6 8.3 %all-to-all-start = ((bf16[1,16,256,256]{3,1,0,2:T(8,128)(2,1)}), bf16[1,16,256,256]{3,1,0,2:T(8,128)(2,1)S(1)}, u32[]{:S(2)}, u32[]{:S(2)}) async-start(bf16[1,16,256,256]{3,1,0,2:T(8,128)(2,1)} %copy.76), calls=%async_computation | async-start | bytes 4194304 | tf_op jit(solution)/shard_map/all_to_all | solution.py:57
  19.0 1.1 negate_convert_fusion
  20.1 0.2 fusion.79
  20.2 41.8 %all-to-all-done = bf16[1,16,256,256]{3,1,0,2:T(8,128)(2,1)S(1)} async-done(((bf16[1,16,256,256]{3,1,0,2:T(8,128)(2,1)}), bf16[1,16,256,256]{3,1,0,2:T(8,128)(2,1)S(1)}, u32[]{:S(2)}, u32[]{:S(2)}) %all-to-all-start) | async-done | bytes 2097184 | tf_op jit(solution)/shard_map/all_to_all | solution.py:57
  62.0 0.7 copy.77
  62.7 1.2 copy.78
  63.9 1.3 fusion.25
  65.2 1.5 fusion.14
  66.6 0.4 fusion
  67.0 0.7 fusion.49
  67.7 0.7 fusion.48
  68.5 0.7 fusion.47
  69.2 0.7 fusion.46
  69.9 0.7 fusion.45
  70.6 0.7 fusion.44
  71.3 0.7 fusion.43
  72.1 0.7 fusion.42
  72.8 0.7 fusion.41
  73.5 0.7 fusion.40
  74.2 0.7 fusion.39
  74.9 0.7 fusion.38
  75.7 0.7 fusion.37
  76.4 0.7 fusion.36
  77.1 0.7 fusion.35
  77.8 0.7 bitcast_dynamic-update-slice_fusion
  78.5 10.1 %all-to-all-start.1 = ((bf16[16,2,1,16,16,256]{5,3,4,1,2,0:T(8,128)(2,1)}), bf16[16,2,1,16,16,256]{5,3,4,1,2,0:T(8,128)(2,1)}, u32[]{:S(2)}, u32[]{:S(2)}) async-start(bf16[16,2,1,16,16,256]{5,3,4,1,2,0:T(8,128)(2,1)} %bitcast_dynamic-update-slice_fusion), calls=%async_computation.1 | async-start | bytes 8388608 | tf_op jit(solution)/shard_map/all_to_all | solution.py:67
  88.6 0.2 all-gather.2.cloned.1.call-start
  88.8 0.5 all-gather.2.cloned.1.call-update
  89.3 1.0 fusion.60
  90.3 1.0 fusion.59
  91.3 1.0 broadcast_multiply_fusion
  92.3 0.1 fusion.23
  92.3 0.9 maximum_bitcast_fusion
  93.2 0.2 fusion.77
  93.4 11.6 %all-gather.2.cloned.1.call-done = bf16[2,16,256,256]{3,2,1,0:T(8,128)(2,1)} async-done(((bf16[2,16,256,128]{3,2,1,0:T(8,128)(2,1)}), bf16[2,16,256,256]{3,2,1,0:T(8,128)(2,1)}) %all-gather.2.cloned.1.call-update) | async-done | bytes 4194320 | tf_op jit(solution)/shard_map/all_gather | solution.py:43
  105.0 6.5 %convert_element_type.144 = f32[2,16,256,256]{3,2,1,0:T(8,128)} convert(bf16[2,16,256,256]{3,2,1,0:T(8,128)(2,1)} %all-gather.2.cloned.1.call-done) | non-fusion elementwise | flops 2097152 | bytes 12582912 | tf_op jit(solution)/shard_map/convert_element_type | solution.py:43
  111.5 55.5 %all-to-all-done.1 = bf16[16,2,1,16,16,256]{5,3,4,1,2,0:T(8,128)(2,1)} async-done(((bf16[16,2,1,16,16,256]{5,3,4,1,2,0:T(8,128)(2,1)}), bf16[16,2,1,16,16,256]{5,3,4,1,2,0:T(8,128)(2,1)}, u32[]{:S(2)}, u32[]{:S(2)}) %all-to-all-start.1) | async-done | bytes 4194336 | tf_op jit(solution)/shard_map/all_to_all | solution.py:67
  167.0 5.7 %copy.94 = bf16[2,1,16,16,16,256]{5,4,3,2,0,1:T(8,128)(2,1)} copy(bf16[2,1,16,16,16,256]{5,2,4,0,1,3:T(8,128)(2,1)} %bitcast.47) | data formatting | bytes 8388608 | tf_op jit(solution)/shard_map/reshape | solution.py:66
  172.6 0.0 slice-start
  172.6 0.0 slice-start.1
  172.6 4.7 %convert_bitcast_fusion.1 = (f32[2,1,16,256,256]{4,3,2,0,1:T(8,128)S(1)}, f32[2,1,16,256,256]{4,3,2,1,0:T(8,128)S(1)}) fusion(bf16[2,16,256,256]{3,2,1,0:T(8,128)(2,1)} %bitcast.186, bf16[1,256,2,256]{1,3,2,0:T(8,128)(2,1)S(1)} %get-tuple-element.16, bf16[1,256,2,256]{1,3,2,0:T(8,128)(2,1)S(1)} %get-tuple-element.15), kind=kOutput, calls=%fused_computation.1 | convolution fusion | flops 2151940096 | bytes 21495808 | tf_op jit(solution)/shard_map/rbknc,rnsj->sbkjc/dot_general | solution.py:70
  177.3 0.0 slice-done
  177.3 0.0 slice-done.1
  177.4 2.9 subtract_convert_fusion.1
  180.3 4.1 %fusion.9 = f32[2,1,16,256,256]{4,3,2,0,1:T(8,128)S(1)} fusion(bf16[1,16,256,256]{3,2,1,0:T(8,128)(2,1)} %get-tuple-element.6, bf16[1,16,256,256]{3,2,1,0:T(8,128)(2,1)S(1)} %get-tuple-element.5, f32[1,256,2,256]{1,3,2,0:T(8,128)} %get-tuple-element.14, f32[1,256,2,256]{1,3,2,0:T(8,128)S(1)} %get-tuple-element.13), kind=kOutput, calls=%fused_computation.26 | convolution fusion | flops 2150367232 | bytes 13631488 | tf_op jit(solution)/shard_map/rbkjc,rjsn->sbknc/dot_general | solution.py:77
  184.4 1.5 subtract_convert_fusion
  185.9 0.4 pad_maximum_fusion.2
  186.3 4.4 %copy.100 = bf16[2,1,16,256,256]{4,2,0,1,3:T(8,128)(2,1)} copy(bf16[2,1,16,256,256]{4,3,2,0,1:T(8,128)(2,1)S(1)} %pad_maximum_fusion.2) | data formatting | bytes 8388608 | tf_op jit(solution)/shard_map/stack | solution.py:87
  190.7 19.4 %all-to-all-start.2 = ((bf16[2,1,16,256,256]{4,2,0,1,3:T(8,128)(2,1)}), bf16[2,1,16,256,256]{4,2,0,1,3:T(8,128)(2,1)}, u32[]{:S(2)}, u32[]{:S(2)}) async-start(bf16[2,1,16,256,256]{4,2,0,1,3:T(8,128)(2,1)} %copy.100), calls=%async_computation.2 | async-start | bytes 8388608 | tf_op jit(solution)/shard_map/all_to_all | solution.py:88
  210.1 1.0 sine_negate_fusion
  211.1 77.4 %all-to-all-done.2 = bf16[2,1,16,256,256]{4,2,0,1,3:T(8,128)(2,1)} async-done(((bf16[2,1,16,256,256]{4,2,0,1,3:T(8,128)(2,1)}), bf16[2,1,16,256,256]{4,2,0,1,3:T(8,128)(2,1)}, u32[]{:S(2)}, u32[]{:S(2)}) %all-to-all-start.2) | async-done | bytes 4194336 | tf_op jit(solution)/shard_map/all_to_all | solution.py:88
  288.5 0.0 copy-start
  288.5 2.7 copy.101
  291.3 0.0 copy-done
  291.3 1.3 fusion.16
  292.6 1.2 copy.102
  293.8 67.5 %all_to_all.50 = bf16[1,256,16,256]{3,2,0,1:T(8,128)(2,1)S(1)} all-to-all(bf16[1,256,16,256]{3,2,0,1:T(8,128)(2,1)S(1)} %copy.102), channel_id=1, replica_groups=mesh['seq'=16,'bat'=2] {'seq'}, dimensions={1} | all-to-all | bytes 4194304 | tf_op jit(solution)/shard_map/all_to_all | solution.py:93
  361.3 1.5 copy.103
  (2 shorter events, 0.0 us)
Async XLA Ops:
  10.6 51.4 %all-to-all-start = ((bf16[1,16,256,256]{3,1,0,2:T(8,128)(2,1)}), bf16[1,16,256,256]{3,1,0,2:T(8,128)(2,1)S(1)}, u32[]{:S(2)}, u32[]{:S(2)}) async-start(bf16[1,16,256,256]{3,1,0,2:T(8,128)(2,1)} %copy.76), calls=%async_computation | async-start | bytes 4194304 | tf_op jit(solution)/shard_map/all_to_all | solution.py:57
  78.5 88.5 %all-to-all-start.1 = ((bf16[16,2,1,16,16,256]{5,3,4,1,2,0:T(8,128)(2,1)}), bf16[16,2,1,16,16,256]{5,3,4,1,2,0:T(8,128)(2,1)}, u32[]{:S(2)}, u32[]{:S(2)}) async-start(bf16[16,2,1,16,16,256]{5,3,4,1,2,0:T(8,128)(2,1)} %bitcast_dynamic-update-slice_fusion), calls=%async_computation.1 | async-start | bytes 8388608 | tf_op jit(solution)/shard_map/all_to_all | solution.py:67
  88.6 16.4 %all-gather.2.cloned.1.call-start = ((), (), s32[]{:S(2)}) async-start(), calls=%async_computation.4 | async-start | bytes 6291456 | tf_op jit(solution)/shard_map/all_gather | solution.py:43
  172.6 4.7 %slice-start = ((s8[8388608]{0:T(1024)(128)(4,1)}), s8[4194304]{0:T(1024)(128)(4,1)S(1)}, s32[]{:S(2)}) async-start(s8[8388608]{0:T(1024)(128)(4,1)} %bitcast.181), calls=%async_computation.5 | async-start | bytes 8388608
  172.6 4.7 %slice-start.1 = ((s8[8388608]{0:T(1024)(128)(4,1)}), s8[4194304]{0:T(1024)(128)(4,1)S(1)}, s32[]{:S(2)}) async-start(s8[8388608]{0:T(1024)(128)(4,1)} %bitcast.181), calls=%async_computation.6 | async-start | bytes 8388608
  190.7 97.9 %all-to-all-start.2 = ((bf16[2,1,16,256,256]{4,2,0,1,3:T(8,128)(2,1)}), bf16[2,1,16,256,256]{4,2,0,1,3:T(8,128)(2,1)}, u32[]{:S(2)}, u32[]{:S(2)}) async-start(bf16[2,1,16,256,256]{4,2,0,1,3:T(8,128)(2,1)} %copy.100), calls=%async_computation.2 | async-start | bytes 8388608 | tf_op jit(solution)/shard_map/all_to_all | solution.py:88
  288.5 2.8 copy-start
Sparse Core Ops, SparseCore 0:
  90.9 13.9 all-gather.1
